TPU v7x, 32 devices: a whole 2x2x4 slice. The times are simulated.
32 devices in a mesh: dp: 4 (over y, x), context: 4 (over z), head: 2 (over core).
Axes of the slice: x: 2, y: 2, z: 4, core: 2. Of those that a mesh axis runs over, the one named last changes fastest.
Arguments:
- tokens: bfloat16 [4, 2, 512, 4096], P('dp', None, 'context', 'head'), may hold values from -7 to 7
- queries: bfloat16 [4, 2, 512, 2048], P('dp', None, 'context', 'head'), may hold values from -160 to 160
- grad_out: bfloat16 [4, 2, 512, 2048], P('dp', None, 'context', 'head'), may hold values from -6 to 6
- w_key: bfloat16 [4096, 256], P('context', 'head'), may hold values from -0.09375 to 0.09375
- w_value: bfloat16 [4096, 256], P('context', 'head'), may hold values from -0.09375 to 0.09375
- block_len: int32 [4], P('dp'), may hold values from 8 to 32, as said below
Outputs:
- grad_query: bfloat16 [4, 2, 512, 2048], P('dp', None, 'context', 'head')
- grad_x: bfloat16 [4, 2, 512, 4096], P('dp', None, 'context', 'head')
- grad_wkey: float32 [4096, 256], P('context', 'head')
- grad_wvalue: float32 [4096, 256], P('context', 'head')
Inputs may be any that keep to these rules, and one draw needn't show every extreme that they name: `block_len`: each entry is 8, 16 or 32.
All inputs are finite; a program needn't handle non-finite values.
Results may differ from a plain program's by a relative error of at most 0.025.
Values may be sent and summed in bfloat16 or wider, within the bound.
A program may use at most 64 MiB of HBM per device.

v0:
```python
import math

import jax
import jax.numpy as jnp
from jax import lax
from jax.sharding import PartitionSpec as P

HEAD_DIM = 128


masked_score = -1e30


def score_block(query_rows, key_rows, score_scale):
    return (
        jnp.einsum("ikgd,jkd->kgij", query_rows, key_rows, preferred_element_type=jnp.float32)
        * score_scale
    )


def visible_mask(query_pos, key_pos, block_size, strict):
    query_block = query_pos // block_size
    key_block = key_pos // block_size
    if strict:
        return key_block[None, :] < query_block[:, None]
    return key_block[None, :] <= query_block[:, None]


def forward_step(carried, query_rows, key_rows, value_rows, allowed_mask, score_scale):
    row_peak, row_total, weighted = carried
    logits = jnp.where(allowed_mask, score_block(query_rows, key_rows, score_scale), masked_score)
    new_peak = jnp.maximum(row_peak, jnp.max(logits, axis=-1))
    shrink = jnp.exp(row_peak - new_peak)
    weights = jnp.where(allowed_mask, jnp.exp(logits - new_peak[..., None]), 0.0)
    row_total = row_total * shrink + jnp.sum(weights, axis=-1)
    update = jnp.einsum(
        "kgij,jkd->kgid",
        weights.astype(jnp.bfloat16),
        value_rows,
        preferred_element_type=jnp.float32,
    )
    return (new_peak, row_total, weighted * shrink[..., None] + update)


def backward_step(
    query_rows, grad_rows, key_rows, value_rows, allowed_mask, log_total, row_delta, score_scale
):
    logits = jnp.where(allowed_mask, score_block(query_rows, key_rows, score_scale), masked_score)
    probs = jnp.exp(logits - log_total[..., None])
    probs_half = probs.astype(jnp.bfloat16)
    grad_probs = jnp.einsum(
        "ikgd,jkd->kgij", grad_rows, value_rows, preferred_element_type=jnp.float32
    )
    grad_logits = (probs * (grad_probs - row_delta[..., None])).astype(jnp.bfloat16)
    grad_rows_query = jnp.einsum(
        "kgij,jkd->ikgd", grad_logits, key_rows, preferred_element_type=jnp.float32
    )
    grad_key = (
        jnp.einsum("kgij,ikgd->jkd", grad_logits, query_rows, preferred_element_type=jnp.float32)
        * score_scale
    )
    grad_value = jnp.einsum(
        "kgij,ikgd->jkd", probs_half, grad_rows, preferred_element_type=jnp.float32
    )
    return (grad_rows_query, grad_key, grad_value)


def finish_rows(carried, grad_rows):
    row_peak, row_total, weighted = carried
    outputs = weighted / row_total[..., None]
    row_delta = jnp.einsum("ikgd,kgid->kgi", grad_rows.astype(jnp.float32), outputs)
    return (row_peak + jnp.log(row_total), row_delta)


def per_device(tokens, queries, grad_out, w_key, w_value, block_len):
    cycle_size = lax.axis_size("context")
    my_index = lax.axis_index("context")
    shard_rows = tokens.shape[2]
    kv_width = w_key.shape[1]
    kv_local = kv_width // HEAD_DIM
    query_width = queries.shape[3]
    group_size = query_width // HEAD_DIM // kv_local
    score_scale = 1.0 / math.sqrt(HEAD_DIM)
    block_size = block_len[0]
    local_pos = lax.iota(jnp.int32, shard_rows)
    span_rows = min(cycle_size * shard_rows, max(512, shard_rows))
    full_tokens = lax.all_gather(
        tokens[0].reshape(2 * shard_rows, tokens.shape[3]), "head", axis=1, tiled=True
    )
    weight_pair = jnp.concatenate([w_key, w_value], axis=1)
    columns = full_tokens
    projected = jnp.dot(
        columns,
        lax.all_gather(weight_pair, "context", axis=0, tiled=True),
        preferred_element_type=jnp.float32,
    ).astype(jnp.bfloat16)
    clean_pairs = projected[:shard_rows]
    q_clean = queries[0, 0].reshape(shard_rows, kv_local, group_size, HEAD_DIM)
    g_clean = grad_out[0, 0].reshape(shard_rows, kv_local, group_size, HEAD_DIM)
    noisy_bundle = jnp.concatenate([queries[0, 1], grad_out[0, 1], projected[shard_rows:]], axis=1)
    q_noisy = noisy_bundle[:, :query_width].reshape(shard_rows, kv_local, group_size, HEAD_DIM)
    g_noisy = noisy_bundle[:, query_width : 2 * query_width].reshape(
        shard_rows, kv_local, group_size, HEAD_DIM
    )
    k_noisy = noisy_bundle[:, 2 * query_width : 2 * query_width + kv_width].reshape(
        shard_rows, kv_local, HEAD_DIM
    )
    v_noisy = noisy_bundle[:, 2 * query_width + kv_width :].reshape(shard_rows, kv_local, HEAD_DIM)
    clean_pos = my_index * shard_rows + local_pos
    noisy_pos = my_index * shard_rows + local_pos
    own_block = local_pos // block_size
    same_block = own_block[None, :] == own_block[:, None]
    clean_limit = (my_index + 1) * shard_rows
    noisy_limit = (my_index + 1) * shard_rows
    state_shape = (kv_local, group_size, shard_rows)
    empty_state = (
        jnp.full(state_shape, masked_score, jnp.float32),
        jnp.zeros(state_shape, jnp.float32),
        jnp.zeros(state_shape + (HEAD_DIM,), jnp.float32),
    )
    noisy_start = forward_step(empty_state, q_noisy, k_noisy, v_noisy, same_block, score_scale)
    block_turns = (jnp.maximum(clean_limit, noisy_limit) + span_rows - 1) // span_rows

    def split_pairs(pair_rows):
        count_rows = pair_rows.shape[0]
        key_rows = pair_rows[:, :kv_width].reshape(count_rows, kv_local, HEAD_DIM)
        value_rows = pair_rows[:, kv_width:].reshape(count_rows, kv_local, HEAD_DIM)
        return (key_rows, value_rows)

    carried = (empty_state, noisy_start)
    pair_rows = lax.all_gather(clean_pairs, "context", axis=0, tiled=True)
    first_row = jnp.int32(0)
    key_rows, value_rows = split_pairs(pair_rows)
    key_pos = lax.iota(jnp.int32, pair_rows.shape[0])
    clean_mask = visible_mask(clean_pos, key_pos, block_size, False)
    noisy_mask = visible_mask(noisy_pos, key_pos, block_size, True)

    def clean_update():
        return forward_step(carried[0], q_clean, key_rows, value_rows, clean_mask, score_scale)

    def clean_keep():
        return carried[0]

    def noisy_update():
        return forward_step(carried[1], q_noisy, key_rows, value_rows, noisy_mask, score_scale)

    def noisy_keep():
        return carried[1]

    clean_state = lax.cond(first_row < clean_limit, clean_update, clean_keep)
    noisy_state = lax.cond(first_row < noisy_limit, noisy_update, noisy_keep)
    clean_lse, clean_delta = finish_rows(clean_state, g_clean)
    noisy_lse, noisy_delta = finish_rows(noisy_state, g_noisy)
    pairs_back = lax.all_gather(clean_pairs, "context", axis=0, tiled=True)
    query_zero = jnp.zeros((shard_rows, kv_local, group_size, HEAD_DIM), jnp.float32)

    def backward_turn(turn_index, carried):
        query_grads, pair_total = carried
        first_row = turn_index * span_rows
        pair_rows = lax.dynamic_slice_in_dim(pairs_back, first_row, span_rows, 0)
        key_rows, value_rows = split_pairs(pair_rows)
        key_pos = first_row + lax.iota(jnp.int32, span_rows)
        clean_mask = visible_mask(clean_pos, key_pos, block_size, False)
        noisy_mask = visible_mask(noisy_pos, key_pos, block_size, True)
        pair_zero = jnp.zeros((span_rows, kv_local, HEAD_DIM), jnp.float32)

        def clean_work():
            return backward_step(
                q_clean,
                g_clean,
                key_rows,
                value_rows,
                clean_mask,
                clean_lse,
                clean_delta,
                score_scale,
            )

        def noisy_work():
            return backward_step(
                q_noisy,
                g_noisy,
                key_rows,
                value_rows,
                noisy_mask,
                noisy_lse,
                noisy_delta,
                score_scale,
            )

        def no_work():
            return (query_zero, pair_zero, pair_zero)

        clean_dq, clean_dk, clean_dv = lax.cond(first_row < clean_limit, clean_work, no_work)
        noisy_dq, noisy_dk, noisy_dv = lax.cond(first_row < noisy_limit, noisy_work, no_work)
        pair_grads = jnp.concatenate(
            [
                (clean_dk + noisy_dk).reshape(span_rows, kv_width),
                (clean_dv + noisy_dv).reshape(span_rows, kv_width),
            ],
            axis=1,
        )
        previous = lax.dynamic_slice_in_dim(pair_total, first_row, span_rows, 0)
        pair_total = lax.dynamic_update_slice_in_dim(
            pair_total, previous + pair_grads, first_row, 0
        )
        return ((query_grads[0] + clean_dq, query_grads[1] + noisy_dq), pair_total)

    pair_empty = jnp.zeros((cycle_size * shard_rows, 2 * kv_width), jnp.float32)
    query_grads, pair_total = lax.fori_loop(
        0, block_turns, backward_turn, ((query_zero, query_zero), pair_empty)
    )
    clean_pair_grads = lax.psum_scatter(
        pair_total.astype(jnp.bfloat16), "context", scatter_dimension=0, tiled=True
    )
    own_dq, own_dk, own_dv = backward_step(
        q_noisy, g_noisy, k_noisy, v_noisy, same_block, noisy_lse, noisy_delta, score_scale
    )
    dq_clean = (query_grads[0] * score_scale).astype(jnp.bfloat16).reshape(shard_rows, query_width)
    dq_noisy = (
        ((query_grads[1] + own_dq) * score_scale)
        .astype(jnp.bfloat16)
        .reshape(shard_rows, query_width)
    )
    noisy_pair = jnp.concatenate(
        [own_dk.reshape(shard_rows, kv_width), own_dv.reshape(shard_rows, kv_width)], axis=1
    ).astype(jnp.bfloat16)
    return_bundle = jnp.concatenate([dq_noisy, noisy_pair], axis=1)
    dq_noisy = return_bundle[:, :query_width]
    noisy_pair = return_bundle[:, query_width:]
    pair_grads = jnp.concatenate([clean_pair_grads, noisy_pair], axis=0)
    input_terms = jnp.einsum(
        "tc,rc->tr",
        pair_grads,
        lax.all_gather(weight_pair, "context", axis=0, tiled=True),
        preferred_element_type=jnp.float32,
    )
    grad_x = lax.psum_scatter(
        input_terms.astype(jnp.bfloat16), "head", scatter_dimension=1, tiled=True
    ).reshape(tokens.shape)
    columns = full_tokens
    weight_local = lax.psum_scatter(
        jnp.einsum("tr,tc->rc", columns, pair_grads, preferred_element_type=jnp.float32).astype(
            jnp.bfloat16
        ),
        "context",
        scatter_dimension=0,
        tiled=True,
    )
    weight_sums = lax.psum(weight_local, "dp").astype(jnp.float32)
    grad_query = jnp.stack([dq_clean, dq_noisy])[None]
    return (grad_query, grad_x, weight_sums[:, :kv_width], weight_sums[:, kv_width:])


def solution(mesh):
    placed = (
        P("dp", None, "context", "head"),
        P("dp", None, "context", "head"),
        P("dp", None, "context", "head"),
        P("context", "head"),
        P("context", "head"),
        P("dp"),
    )
    return jax.shard_map(
        per_device,
        mesh=mesh,
        in_specs=placed,
        out_specs=(
            P("dp", None, "context", "head"),
            P("dp", None, "context", "head"),
            P("context", "head"),
            P("context", "head"),
        ),
        check_vma=False,
    )
```

profile of v0, /device:TPU:0, one launch (start us, length us, event | category | flops | bytes accessed | tf_op | source)
XLA Modules:
  0.0 246.0 jit_solution(10116017296213389250)
XLA Ops:
  8.0 1.9 pad_maximum_fusion
  10.9 0.9 copy.91
  11.9 0.9 copy.89
  14.0 8.9 %all-gather.5.cloned.1.call-done = bf16[256,4096]{1,0:T(8,128)(2,1)} async-done(((bf16[256,2048]{1,0:T(8,128)(2,1)}), bf16[256,4096]{1,0:T(8,128)(2,1)}) %all-gather.5.cloned.1.call-update) | async-done | bytes 2097168 | tf_op jit(solution)/shard_map/all_gather | solution.py:87
  22.9 49.0 %all-gather.3.cloned.1.call-done = bf16[4096,256]{1,0:T(8,128)(2,1)} async-done(((bf16[1024,256]{1,0:T(8,128)(2,1)}), bf16[4096,256]{1,0:T(8,128)(2,1)}) %all-gather.3.cloned.1.call-update) | async-done | bytes 2097168 | tf_op jit(solution)/shard_map/all_gather | solution.py:94
  71.9 3.0 %fusion.88 = bf16[256,256]{0,1:T(8,128)(2,1)S(1)} fusion(bf16[4096,256]{1,0:T(8,128)(2,1)} %all-gather.3.cloned.1.call-done, bf16[256,4096]{1,0:T(8,128)(2,1)} %all-gather.5.cloned.1.call-done), kind=kOutput, calls=%fused_computation.128 | convolution fusion | flops 536936448 | bytes 4325376 | tf_op jit(solution)/shard_map/dot_general | solution.py:92
  74.9 13.4 %all_gather.13 = bf16[512,256]{0,1:T(8,128)(2,1)S(1)} all-gather(bf16[128,256]{0,1:T(8,128)(2,1)S(1)} %slice.67), channel_id=1, replica_groups=mesh['dp'=4,'context'=4,'head'=2] {'context'}, dimensions={0}, use_global_device_ids=true | all-gather | bytes 327680 | tf_op jit(solution)/shard_map/all_gather | solution.py:154
  91.2 2.9 %conditional.4 = (f32[1,8,128]{2,1,0:T(8,128)S(1)}, f32[1,8,128]{2,1,0:T(8,128)S(1)}, f32[1,8,128,128]{3,2,1,0:T(8,128)S(1)}, f32[1,8,128]{2,1,0:T(8,128)S(1)}) conditional(s32[]{:T(128)} %convert_element_type.73, () %tuple.57, (s32[512]{0:T(512)S(1)}, s32[128,512]{0,1:T(8,128)S(1)}, bf16[512,1,128]{0,2,1:T(8,128)(2,1)S(1)}, ...), branch_computations={%region_0.1_spmd, %region_1.4_spmd} | conditional | flops 275452928 | bytes 7919648 | solution.py:150
  92.4 1.7 fusion.7
  95.1 2.9 %conditional.5 = (f32[1,8,128]{2,1,0:T(8,128)S(1)}, f32[1,8,128]{2,1,0:T(8,128)S(1)}, f32[1,8,128,128]{3,2,1,0:T(8,128)S(1)}, f32[1,8,128]{2,1,0:T(8,128)S(1)}) conditional(s32[]{:T(128)} %convert_element_type.73, (f32[1,8,128]{2,1,0:T(8,128)S(1)}, f32[1,8,128]{2,1,0:T(8,128)S(1)}, f32[1,8,128,128]{3,2,1,0:T(8,128)S(1)}) %tuple.59, ...), branch_computations={%region_6.7_spmd, %region_7.10_spmd} | conditional | flops 275581952 | bytes 8460320 | solution.py:151
  95.8 1.7 fusion.26
  99.8 13.3 %while.20 = (s32[]{:T(128)}, f32[128,1,8,128]{3,0,2,1:T(8,128)}, f32[128,1,8,128]{3,0,2,1:T(8,128)S(1)}, f32[512,256]{1,0:T(8,128)S(1)}, s32[]{:T(128)}, /*index...) while((s32[]{:T(128)}, f32[128,1,8,128]{3,0,2,1:T(8,128)}, ...), condition=%wide.region_15.16_spmd.clone.clone, body=%wide.region_10.15_spmd.clone.clone.sunk | while | flops 1350440704 | bytes 32791988 | solution.py:210
  101.4 1.0 slice_bitcast_fusion.11
  102.4 4.5 %conditional.12 = (f32[128,1,8,128]{3,0,2,1:T(8,128)S(1)}, f32[512,1,128]{2,0,1:T(8,128)S(1)}, f32[512,1,128]{2,0,1:T(8,128)S(1)}) conditional(s32[]{:T(128)} %convert_element_type.129, () %tuple.125, (s32[512]{0:T(512)S(1)}, s32[128,512]{0,1:T(8,128)S(1)}, bf16[512,1,128]{2,0,1:T(8,128)(2,1)S(1)}, bf16[128,1,8,128]{3,0,2,1:T(8,128)(2,1)}, ...), branch_computations={%region_11.11_spmd, %region_12.12_spmd} | conditional | flops 674889728 | bytes 12331032 | solution.py:194
  102.6 1.5 fusion.45
  105.0 1.4 fusion.48
  106.9 1.9 add.307
  108.8 4.0 %conditional.13 = (f32[128,1,8,128]{3,0,2,1:T(8,128)S(1)}, f32[512,1,128]{2,0,1:T(8,128)S(1)}, f32[512,1,128]{2,0,1:T(8,128)S(1)}) conditional(s32[]{:T(128)} %convert_element_type.129, () %tuple.127, (s32[512]{0:T(512)S(1)}, s32[128,512]{0,1:T(8,128)S(1)}, bf16[512,1,128]{2,0,1:T(8,128)(2,1)S(1)}, bf16[128,1,8,128]{3,0,2,1:T(8,128)(2,1)}, ...), branch_computations={%region_13.13_spmd, %region_14.14_spmd} | conditional | flops 674889728 | bytes 13379636 | solution.py:195
  108.9 1.5 fusion.61
  114.2 1.4 fusion.87
  116.1 16.7 %reduce-scatter.10.cloned.1.call-done = bf16[128,256]{1,0:T(8,128)(2,1)} async-done(((bf16[512,256]{1,0:T(8,128)(2,1)}), bf16[128,256]{1,0:T(8,128)(2,1)}) %reduce-scatter.10.cloned.1.call-update) | async-done | bytes 65552
  132.8 0.9 copy.132
  133.7 3.7 %fusion.77 = bf16[4096,256]{0,1:T(8,128)(2,1)} fusion(bf16[256,4096]{1,0:T(8,128)(2,1)} %all-gather.5.cloned.1.call-done, bf16[128,128]{0,1:T(8,128)(2,1)S(1)} %fusion.90, bf16[128,128]{0,1:T(8,128)(2,1)S(1)} %fusion.91, bf16[128,256]{0,1:T(8,128)(2,1)S(1)} %copy.132), kind=kOutput, calls=%fused_computation.112 | convolution fusion | flops 538312704 | bytes 4325376 | tf_op jit(solution)/shard_map/tr,tc->rc/dot_general | solution.py:243
  137.5 41.9 %reduce-scatter.8.cloned.1.call-done = bf16[1024,256]{0,1:T(8,128)(2,1)} async-done(((bf16[4096,256]{0,1:T(8,128)(2,1)}), bf16[1024,256]{0,1:T(8,128)(2,1)}) %reduce-scatter.8.cloned.1.call-update) | async-done | bytes 524304 | tf_op jit(solution)/shard_map/reduce_scatter | solution.py:242
  179.5 2.1 convolution_convert_fusion.1
  181.6 1.0 copy-done
  183.3 1.0 fusion.84
  185.2 41.6 %all-reduce.2.cloned.1.call-done = bf16[1024,256]{0,1:T(8,128)(2,1)} async-done(((bf16[1024,256]{0,1:T(8,128)(2,1)}), bf16[1024,256]{0,1:T(8,128)(2,1)}) %all-reduce.2.cloned.1.call-update) | async-done | bytes 524304 | tf_op jit(solution)/shard_map/psum | solution.py:250
  226.9 1.1 fusion.111
  228.0 1.0 copy.104
  229.0 1.0 copy.103
  230.0 9.2 %reduce-scatter.6.cloned.1.call-done = bf16[256,2048]{1,0:T(8,128)(2,1)} async-done(((bf16[256,4096]{1,0:T(8,128)(2,1)}), bf16[256,2048]{1,0:T(8,128)(2,1)}) %reduce-scatter.6.cloned.1.call-update) | async-done | bytes 1048592 | tf_op jit(solution)/shard_map/reduce_scatter | solution.py:238
  (111 shorter events, 19.3 us)
Async XLA Ops:
  7.2 3.5 %copy-start.9 = (bf16[1,2,128,1024]{3,2,1,0:T(8,128)(2,1)S(1)}, bf16[1,2,128,1024]{3,2,1,0:T(8,128)(2,1)}, u32[]{:S(2)}) copy-start(bf16[1,2,128,1024]{3,2,1,0:T(8,128)(2,1)} %param.17) | copy-start | bytes 1572868
  7.2 15.7 %all-gather.5.cloned.1.call-start = ((), (), s32[]{:S(2)}) async-start(), calls=%async_computation.4 | async-start | bytes 3145728 | tf_op jit(solution)/shard_map/all_gather | solution.py:87
  7.9 64.0 %all-gather.3.cloned.1.call-start = ((), (), s32[]{:S(2)}) async-start(), calls=%async_computation.3 | async-start | bytes 2621440 | tf_op jit(solution)/shard_map/all_gather | solution.py:94
  9.8 2.9 %copy-start.10 = (bf16[1,2,128,1024]{3,2,1,0:T(8,128)(2,1)S(1)}, bf16[1,2,128,1024]{3,2,1,0:T(8,128)(2,1)}, u32[]{:S(2)}) copy-start(bf16[1,2,128,1024]{3,2,1,0:T(8,128)(2,1)} %param.18) | copy-start | bytes 1572868
  9.9 122.9 %reduce-scatter.10.cloned.1.call-start = ((), (), s32[]{:S(2)}) async-start(), calls=%async_computation.8 | async-start | bytes 327680
  10.8 84.3 %copy-start.4 = (bf16[1,1,128,1024]{2,3,1,0:T(8,128)(2,1)}, bf16[1,1,128,1024]{2,3,1,0:T(8,128)(2,1)S(1)}, u32[]{:S(2)}) copy-start(bf16[1,1,128,1024]{2,3,1,0:T(8,128)(2,1)S(1)} %copy.135) | copy-start | bytes 786436
  13.0 85.9 %copy-start.6 = (bf16[1,1,128,1024]{2,3,1,0:T(8,128)(2,1)}, bf16[1,1,128,1024]{2,3,1,0:T(8,128)(2,1)S(1)}, u32[]{:S(2)}) copy-start(bf16[1,1,128,1024]{2,3,1,0:T(8,128)(2,1)S(1)} %copy.136) | copy-start | bytes 786436
  74.8 16.4 %copy-start.11 = (bf16[256,256]{0,1:T(8,128)(2,1)}, bf16[256,256]{0,1:T(8,128)(2,1)S(1)}, u32[]{:S(2)}) copy-start(bf16[256,256]{0,1:T(8,128)(2,1)S(1)} %fusion.88) | copy-start | bytes 393220
  90.1 0.8 copy-start.1
  94.1 0.6 copy-start.12
  94.1 0.6 copy-start.14
  98.0 0.7 copy-start.13
  98.1 0.7 copy-start.15
  110.9 1.0 copy-start.3
  113.1 2.5 %copy-start.5 = (bf16[1,1,128,1024]{2,3,1,0:T(8,128)(2,1)S(1)}, bf16[1,1,128,1024]{2,3,1,0:T(8,128)(2,1)}, u32[]{:S(2)}) copy-start(bf16[1,1,128,1024]{2,3,1,0:T(8,128)(2,1)} %copy-done.4) | copy-start | bytes 786436
  113.1 2.7 %copy-start.2 = (f32[1,8,128,128]{2,3,1,0:T(8,128)S(1)}, f32[1,8,128,128]{2,3,1,0:T(8,128)}, u32[]{:S(2)}) copy-start(f32[1,8,128,128]{2,3,1,0:T(8,128)} %copy-done.1) | copy-start | bytes 1572868
  113.1 2.7 %copy-start.7 = (bf16[1,1,128,1024]{2,3,1,0:T(8,128)(2,1)S(1)}, bf16[1,1,128,1024]{2,3,1,0:T(8,128)(2,1)}, u32[]{:S(2)}) copy-start(bf16[1,1,128,1024]{2,3,1,0:T(8,128)(2,1)} %copy-done.6) | copy-start | bytes 786436
  114.1 65.3 %reduce-scatter.8.cloned.1.call-start = ((), (), s32[]{:S(2)}) async-start(), calls=%async_computation.6 | async-start | bytes 2621440 | tf_op jit(solution)/shard_map/reduce_scatter | solution.py:242
  137.4 42.1 %copy-start.8 = (bf16[4096,256]{1,0:T(8,128)(2,1)S(1)}, bf16[4096,256]{1,0:T(8,128)(2,1)}, u32[]{:S(2)}) copy-start(bf16[4096,256]{1,0:T(8,128)(2,1)} %all-gather.3.cloned.1.call-done) | copy-start | bytes 6291460
  137.4 89.4 %all-reduce.2.cloned.1.call-start = ((), (), s32[]{:S(2)}) async-start(), calls=%async_computation.7 | async-start | bytes 1048576 | tf_op jit(solution)/shard_map/psum | solution.py:250
  179.4 59.7 %reduce-scatter.6.cloned.1.call-start = ((), (), s32[]{:S(2)}) async-start(), calls=%async_computation.5 | async-start | bytes 3145728 | tf_op jit(solution)/shard_map/reduce_scatter | solution.py:238
  181.6 1.0 copy-start
Sparse Core Ops, SparseCore 0:
  9.5 13.2 all-gather.4
  25.0 46.8 all-gather.2
  114.3 18.4 reduce-scatter.9
  137.5 41.8 reduce-scatter.7
  182.3 44.5 all-reduce.1
  229.5 9.6 reduce-scatter.5
where the time goes:
time: 247 us; the launch traced here: 246 us
  waiting for transfers between devices  168 us (68%)
  matrix products  24.1 us (10%)
  local copies, waits for them, and re-layouts  15.5 us (6%)
  between operations  15.3 us (6%)
  blocking collectives  13.4 us (5%)
  other arithmetic  9.27 us (4%)
    all_gather x1, waiting for transfers between devices, per_device(): lax.all_gather(weight_pair, 'context', axis=0, tiled=True)  49 us
    reduce_scatter x1, waiting for transfers between devices, per_device(): lax.psum_scatter(jnp.einsum('tr,tc->rc', columns, pair_grads, preferred_e...  41.9 us
    psum x1, waiting for transfers between devices, per_device(): weight_sums = lax.psum(weight_local, 'dp').astype(jnp.float32)  41.6 us
    unnamed x7, waiting for transfers between devices  17.4 us
    all_gather x1, blocking collectives, per_device(): pairs_back = lax.all_gather(clean_pairs, 'context', axis=0, tiled=True)  13.4 us
    unnamed x45, local copies, waits for them, and re-layouts  10.3 us
    reduce_scatter x1, waiting for transfers between devices, per_device(): lax.psum_scatter(input_terms.astype(jnp.bfloat16), 'head', scatter_dimens...  9.19 us
    all_gather x1, waiting for transfers between devices, per_device(): lax.all_gather(tokens[0].reshape(2 * shard_rows, tokens.shape[3]), 'head'...  8.85 us
  transfers between devices with their start and end apart: 6, of which 6 were waited for; matrix products, arithmetic and copies ran while one was open for 6% of the time, Pallas kernels for 0%

commit v1 on v0

v1 whole, which is shorter than its diff:
```python
import functools
import math

import jax
import jax.numpy as jnp
from jax import lax
from jax.experimental import pallas as pl
from jax.experimental.pallas import tpu as pltpu
from jax.sharding import PartitionSpec as P

HEAD_DIM = 128
MASKED = -1e30
MESH = pl.DeviceIdType.MESH
NT = (((1,), (1,)), ((), ()))


def near_first(count):
    order = []
    for step in range(1, count):
        for offset in (step, count - step):
            if offset not in order:
                order.append(offset)
    return order


def dot(left, right):
    return jnp.dot(left, right, preferred_element_type=jnp.float32)


def dot_nt(left, right):
    return lax.dot_general(left, right, NT, preferred_element_type=jnp.float32)


def fused_kernel(
    n, m, share, early,
    blk_ref, tok_ref, q_ref, g_ref, wk_ref, wv_ref,
    dq_ref, gx_ref, gw_ref,
    tokf, wf, wo, kv, kvn, kt, knt, dkv, dn, pgp, pin, pga, pgo, tokd, gsum, rp, rin, rall,
    loc_sem, tok_sem, wz_s, wz_r, wd_s, wd_r, wx_s, wx_r, wo_sem, kv_s, kv_r,
    td_s, td_r, tf_s, tf_r, pp_s, pp_r, pn_s, pn_r, pc_s, pc_r, po_sem, rs_s, rs_r, ra_s, ra_r,
):
    me_dp = lax.axis_index("dp")
    me = lax.axis_index("context")
    head = lax.axis_index("head")
    other = 1 - head
    rows2, features = tok_ref.shape
    rows = rows2 // 2
    wrows = wk_ref.shape[0]
    half = n // 2
    score_scale = 1.0 / math.sqrt(HEAD_DIM)
    sends = []

    def copy_of(src, dst, send_sem, recv_sem, **device):
        return pltpu.make_async_remote_copy(
            src_ref=src, dst_ref=dst, send_sem=send_sem, recv_sem=recv_sem,
            device_id=device, device_id_type=MESH,
        )

    def put(src, dst, send_sem, recv_sem, **device):
        copy = copy_of(src, dst, send_sem, recv_sem, **device)
        copy.start()
        sends.append(copy)

    def arrived(dst, send_sem, recv_sem):
        copy_of(dst, dst, send_sem, recv_sem, head=other).wait_recv()

    ctx_peers = [(off, lax.rem(me + off, n)) for off in near_first(n)]
    dp_peers = [(off, lax.rem(me_dp + off, m)) for off in near_first(m)]

    own_copies = [
        pltpu.make_async_copy(wk_ref, wf.at[me, :, pl.ds(0, HEAD_DIM)], loc_sem.at[0]),
        pltpu.make_async_copy(wv_ref, wf.at[me, :, pl.ds(HEAD_DIM, HEAD_DIM)], loc_sem.at[1]),
        pltpu.make_async_copy(tok_ref, tokf.at[head], loc_sem.at[2]),
    ]
    for copy in own_copies:
        copy.start()

    barrier = pltpu.get_barrier_semaphore()
    for _, peer in ctx_peers:
        pl.semaphore_signal(barrier, inc=1, device_id={"context": peer}, device_id_type=MESH)
    for _, peer in dp_peers:
        pl.semaphore_signal(barrier, inc=1, device_id={"dp": peer}, device_id_type=MESH)
    pl.semaphore_signal(barrier, inc=1, device_id={"head": other}, device_id_type=MESH)
    pl.semaphore_wait(barrier, n + m - 1)

    put(tok_ref, tokf.at[head], tok_sem.at[0], tok_sem.at[1], head=other)
    own_copies[0].wait()
    own_copies[1].wait()
    shared = pl.ds(pl.multiple_of(me_dp * share, 16), share)
    direct_rows = wrows - m * share
    direct = pl.ds(m * share, direct_rows)
    for off, peer in ctx_peers:
        part = wf.at[me, shared]
        put(part, part, wz_s.at[off], wz_r.at[me], context=peer)
    if direct_rows:
        for off, peer in ctx_peers:
            part = wf.at[me, direct]
            put(part, part, wd_s.at[off], wd_r.at[me], context=peer)
    own_copies[2].wait()
    arrived(tokf.at[other], tok_sem.at[0], tok_sem.at[1])

    def token_block(owner):
        column = pl.multiple_of(lax.rem(owner, half) * wrows, 128)
        return owner // half, pl.ds(column, wrows)

    def token_rows(core, part):
        start = 0 if part == 0 else early
        count = early if part == 0 else rows - early
        return pl.ds(pl.multiple_of(core * rows + start, 16), count)

    def send_tokens(part):
        span = token_rows(head, part)
        for off, peer in ctx_peers:
            side, columns = token_block(peer)
            put(
                tokf.at[side, span, columns], tokd.at[me, span],
                td_s.at[part, off], td_r.at[part, me], context=peer,
            )

    my_side, my_columns = token_block(me)
    own_tokens = pltpu.make_async_copy(tokf.at[my_side, :, my_columns], tokd.at[me], loc_sem.at[3])
    own_tokens.start()
    for off, src in ctx_peers:
        part = wf.at[src, shared]
        arrived(part, wz_s.at[off], wz_r.at[src])
        for dp_off, peer in dp_peers:
            put(part, part, wx_s.at[src, dp_off], wx_r.at[src, me_dp], dp=peer)
    send_tokens(0)

    projected = dot(tokf[my_side, :, my_columns], wf[me])
    for off, src in ctx_peers:
        if direct_rows:
            arrived(wf.at[src, direct], wd_s.at[off], wd_r.at[src])
        for dp_off, peer in dp_peers:
            theirs = pl.ds(pl.multiple_of(peer * share, 16), share)
            arrived(wf.at[src, theirs], wx_s.at[src, dp_off], wx_r.at[src, peer])
        side, columns = token_block(src)
        projected += dot(tokf[side, :, columns], wf[src])
    pairs = projected.astype(jnp.bfloat16)
    my_rows = pl.ds(pl.multiple_of(me * rows, rows), rows)
    kv[my_rows, :] = pairs[:rows]
    kvn[...] = pairs[rows:]
    for off, peer in ctx_peers:
        put(kv.at[my_rows], kv.at[my_rows], kv_s.at[off], kv_r.at[me], context=peer)
    put(wf.at[pl.ds(other * half, half)], wo, wo_sem.at[0], wo_sem.at[1], head=other)
    send_tokens(1)

    block = blk_ref[0]
    total_rows = n * rows
    lane = lax.broadcasted_iota(jnp.int32, (1, rows2), 1)
    noisy_lane = lane >= rows
    position = me * rows + jnp.where(noisy_lane, lane - rows, lane)
    block_start = position & (-block)
    limit = jnp.where(noisy_lane, block_start, block_start + block)
    dkv[...] = jnp.zeros_like(dkv)
    dn[...] = jnp.zeros_like(dn)
    knt[...] = kvn[:, :HEAD_DIM].T
    for off, src in ctx_peers:
        span = pl.ds(pl.multiple_of(src * rows, rows), rows)
        arrived(kv.at[span], kv_s.at[off], kv_r.at[src])
    kt[...] = kv[:, :HEAD_DIM].T

    def head_turn(turn, carry):
        columns = pl.ds(pl.multiple_of(turn * HEAD_DIM, HEAD_DIM), HEAD_DIM)
        q = q_ref[:, columns]
        g = g_ref[:, columns]
        keys = kv[:, :HEAD_DIM]
        values = kv[:, HEAD_DIM:]
        own_keys = kvn[:, :HEAD_DIM]
        own_values = kvn[:, HEAD_DIM:]
        key_pos = lax.broadcasted_iota(jnp.int32, (total_rows, rows2), 0)
        near = lax.broadcasted_iota(jnp.int32, (rows, rows), 0)
        same = (near ^ lax.broadcasted_iota(jnp.int32, (rows, rows), 1)) < block
        s = jnp.where(key_pos < limit, dot_nt(keys, q) * score_scale, MASKED)
        s_own = jnp.where(same, dot_nt(own_keys, q[rows:]) * score_scale, MASKED)
        peak = jnp.max(s, axis=0, keepdims=True)
        peak_own = jnp.maximum(peak[:, rows:], jnp.max(s_own, axis=0, keepdims=True))
        peak = jnp.concatenate([peak[:, :rows], peak_own], axis=1)
        e = jnp.exp(s - peak)
        e_own = jnp.exp(s_own - peak_own)
        total = jnp.sum(e, axis=0, keepdims=True)
        total_own = total[:, rows:] + jnp.sum(e_own, axis=0, keepdims=True)
        inverse = 1.0 / jnp.concatenate([total[:, :rows], total_own], axis=1)
        p = e * inverse
        p_own = e_own * inverse[:, rows:]
        p_half = p.astype(jnp.bfloat16)
        p_half_own = p_own.astype(jnp.bfloat16)
        gp = dot_nt(values, g)
        gp_own = dot_nt(own_values, g[rows:])
        delta = jnp.sum(p_half.astype(jnp.float32) * gp, axis=0, keepdims=True)
        delta_own = delta[:, rows:] + jnp.sum(
            p_half_own.astype(jnp.float32) * gp_own, axis=0, keepdims=True
        )
        delta = jnp.concatenate([delta[:, :rows], delta_own], axis=1)
        ds = (p * (gp - delta)).astype(jnp.bfloat16)
        ds_own = (p_own * (gp_own - delta_own)).astype(jnp.bfloat16)
        dkv[:, :HEAD_DIM] += dot(ds, q)
        dkv[:, HEAD_DIM:] += dot(p_half, g)
        dn[:, :HEAD_DIM] += dot(ds_own, q[rows:])
        dn[:, HEAD_DIM:] += dot(p_half_own, g[rows:])
        dq = dot(kt[...], ds)
        dq_own = dq[:, rows:] + dot(knt[...], ds_own)
        dq_ref[:rows, columns] = (dq[:, :rows] * score_scale).T.astype(jnp.bfloat16)
        dq_ref[rows:, columns] = (dq_own * score_scale).T.astype(jnp.bfloat16)
        return carry

    lax.fori_loop(0, q_ref.shape[1] // HEAD_DIM, head_turn, 0)

    pair_scale = jnp.where(
        lax.broadcasted_iota(jnp.int32, (1, 2 * HEAD_DIM), 1) < HEAD_DIM, score_scale, 1.0
    )
    for block_at in range(n):
        pgp[block_at] = (dkv[block_at * rows : (block_at + 1) * rows] * pair_scale).astype(jnp.bfloat16)
    clean, noisy = pl.ds(0, rows), pl.ds(rows, rows)
    for off, peer in ctx_peers:
        put(pgp.at[peer], pin.at[me], pp_s.at[off], pp_r.at[me], context=peer)
    pga[me, noisy] = (dn[...] * pair_scale).astype(jnp.bfloat16)
    part = pga.at[me, noisy]
    put(part, pgo.at[noisy], po_sem.at[0], po_sem.at[1], head=other)
    for off, peer in ctx_peers:
        put(part, part, pn_s.at[off], pn_r.at[me], context=peer)
    clean_sum = dkv[my_rows, :] * pair_scale
    for off, src in ctx_peers:
        arrived(pin.at[src], pp_s.at[off], pp_r.at[src])
        clean_sum += pin[src].astype(jnp.float32)
    pga[me, clean] = clean_sum.astype(jnp.bfloat16)
    part = pga.at[me, clean]
    for off, peer in ctx_peers:
        put(part, part, pc_s.at[off], pc_r.at[me], context=peer)
    put(part, pgo.at[clean], po_sem.at[2], po_sem.at[3], head=other)

    for off, src in ctx_peers:
        for piece in range(2):
            span = token_rows(head, piece)
            part = tokd.at[src, span]
            arrived(part, td_s.at[piece, off], td_r.at[piece, src])
            put(part, part, tf_s.at[piece, off], tf_r.at[piece, src], head=other)
    own_tokens.wait()
    arrived(wo, wo_sem.at[0], wo_sem.at[1])
    arrived(pgo.at[noisy], po_sem.at[0], po_sem.at[1])
    arrived(pgo.at[clean], po_sem.at[2], po_sem.at[3])

    for at in range(half):
        gx_ref[:, at * wrows : (at + 1) * wrows] = (
            dot_nt(pga[me], wf[head * half + at]) + dot_nt(pgo[...], wo[at])
        ).astype(jnp.bfloat16)

    gw = dot(pga[me].T, tokd[me])
    for off, src in ctx_peers:
        for piece in range(2):
            span = token_rows(other, piece)
            arrived(tokd.at[src, span], tf_s.at[piece, off], tf_r.at[piece, src])
        arrived(pga.at[src, noisy], pn_s.at[off], pn_r.at[src])
        arrived(pga.at[src, clean], pc_s.at[off], pc_r.at[src])
        gw += dot(pga[src].T, tokd[src])

    slab = gw.shape[0] // m
    for at in range(m):
        gsum[at] = gw[at * slab : (at + 1) * slab]
        rp[at] = gw[at * slab : (at + 1) * slab].astype(jnp.bfloat16)
    for off, peer in dp_peers:
        put(rp.at[peer], rin.at[me_dp], rs_s.at[off], rs_r.at[me_dp], dp=peer)
    slab_sum = gsum[me_dp]
    for off, src in dp_peers:
        arrived(rin.at[src], rs_s.at[off], rs_r.at[src])
        slab_sum += rin[src].astype(jnp.float32)
    rall[me_dp] = slab_sum.astype(jnp.bfloat16)
    for off, peer in dp_peers:
        put(rall.at[me_dp], rall.at[me_dp], ra_s.at[off], ra_r.at[me_dp], dp=peer)
    for off, src in dp_peers:
        arrived(rall.at[src], ra_s.at[off], ra_r.at[src])
    for at in range(m):
        gw_ref[at * slab : (at + 1) * slab] = rall[at].astype(jnp.float32)
    for copy in sends:
        copy.wait_send()


def per_device(tokens, queries, grad_out, w_key, w_value, block_len):
    n = lax.axis_size("context")
    m = lax.axis_size("dp")
    rows = tokens.shape[2]
    features = tokens.shape[3]
    wrows, width = w_key.shape
    q_width = queries.shape[3]
    share = wrows * 7 // 8 // m // 16 * 16
    early = rows // 2
    half = n // 2
    pair = 2 * width
    bf16, f32 = jnp.bfloat16, jnp.float32
    vmem = pl.BlockSpec(memory_space=pltpu.VMEM)
    dma = pltpu.SemaphoreType.DMA
    slab = pair // m
    dq, gx, gw = pl.pallas_call(
        functools.partial(fused_kernel, n, m, share, early),
        out_shape=(
            jax.ShapeDtypeStruct((2 * rows, q_width), bf16),
            jax.ShapeDtypeStruct((2 * rows, features), bf16),
            jax.ShapeDtypeStruct((pair, wrows), f32),
        ),
        in_specs=[pl.BlockSpec(memory_space=pltpu.SMEM)] + [vmem] * 5,
        out_specs=(vmem, vmem, vmem),
        scratch_shapes=[
            pltpu.VMEM((2, 2 * rows, features), bf16),
            pltpu.VMEM((n, wrows, pair), bf16),
            pltpu.VMEM((half, wrows, pair), bf16),
            pltpu.VMEM((n * rows, pair), bf16),
            pltpu.VMEM((rows, pair), bf16),
            pltpu.VMEM((width, n * rows), bf16),
            pltpu.VMEM((width, rows), bf16),
            pltpu.VMEM((n * rows, pair), f32),
            pltpu.VMEM((rows, pair), f32),
            pltpu.VMEM((n, rows, pair), bf16),
            pltpu.VMEM((n, rows, pair), bf16),
            pltpu.VMEM((n, 2 * rows, pair), bf16),
            pltpu.VMEM((2 * rows, pair), bf16),
            pltpu.VMEM((n, 2 * rows, wrows), bf16),
            pltpu.VMEM((m, slab, wrows), f32),
            pltpu.VMEM((m, slab, wrows), bf16),
            pltpu.VMEM((m, slab, wrows), bf16),
            pltpu.VMEM((m, slab, wrows), bf16),
            dma((4,)), dma((2,)), dma((n,)), dma((n,)), dma((n,)), dma((n,)),
            dma((n, m)), dma((n, m)), dma((2,)), dma((n,)), dma((n,)),
            dma((2, n)), dma((2, n)), dma((2, n)), dma((2, n)),
            dma((n,)), dma((n,)), dma((n,)), dma((n,)), dma((n,)), dma((n,)),
            dma((4,)), dma((m,)), dma((m,)), dma((m,)), dma((m,)),
        ],
        compiler_params=pltpu.CompilerParams(
            collective_id=0, has_side_effects=True, vmem_limit_bytes=60 * 1024 * 1024
        ),
    )(
        block_len,
        tokens.reshape(2 * rows, features),
        queries.reshape(2 * rows, q_width),
        grad_out.reshape(2 * rows, q_width),
        w_key,
        w_value,
    )
    return (
        dq.reshape(queries.shape),
        gx.reshape(tokens.shape),
        gw[:width].T,
        gw[width:].T,
    )


def solution(mesh):
    placed = (
        P("dp", None, "context", "head"),
        P("dp", None, "context", "head"),
        P("dp", None, "context", "head"),
        P("context", "head"),
        P("context", "head"),
        P("dp"),
    )
    return jax.shard_map(
        per_device,
        mesh=mesh,
        in_specs=placed,
        out_specs=(
            P("dp", None, "context", "head"),
            P("dp", None, "context", "head"),
            P("context", "head"),
            P("context", "head"),
        ),
        check_vma=False,
    )
```

time: 247 us -> 93.1 us (0.38)
  waiting for transfers between devices: 168 us -> 0 us
  Pallas kernels: 0 us -> 86.6 us
  matrix products: 24.1 us -> 0 us
  between operations: 15.3 us -> 1.3 us
  blocking collectives: 13.4 us -> 0 us
  local copies, waits for them, and re-layouts: 15.5 us -> 5.03 us
  other arithmetic: 9.27 us -> 0 us
    pallas_call x0 -> x1, Pallas kernels: none -> 86.6 us  [per_device(): pl.pallas_call(functools.partial(fused_kernel, n, m, share, early), out_s...]
    all_gather x2 -> x0, waiting for transfers between devices: 57.9 us -> none  [the longest x1 49 us: per_device(): lax.all_gather(weight_pair, 'context', axis=0, tiled=True)]
    reduce_scatter x2 -> x0, waiting for transfers between devices: 51.1 us -> none  [the longest x1 41.9 us: per_device(): lax.psum_scatter(jnp.einsum('tr,tc->rc', columns, pair_grads, preferred_e...]
    psum x1 -> x0, waiting for transfers between devices: 41.6 us -> none  [per_device(): weight_sums = lax.psum(weight_local, 'dp').astype(jnp.float32)]
    dot_general x23 -> x0, matrix products: 24.1 us -> none  [the longest x5 4.28 us: score_block(): jnp.einsum('ikgd,jkd->kgij', query_rows, key_rows, preferred_element_type...]
    unnamed x7 -> x0, waiting for transfers between devices: 17.4 us -> none
    all_gather x1 -> x0, blocking collectives: 13.4 us -> none  [per_device(): pairs_back = lax.all_gather(clean_pairs, 'context', axis=0, tiled=True)]
    unnamed x45 -> x8, local copies, waits for them, and re-layouts: 10.3 us -> 3.76 us
  transfers between devices with their start and end apart: 6 -> 0, of which waited for: 6 -> 0; matrix products, arithmetic and copies ran while one was open for 6% -> 0% of each run, Pallas kernels for 0% -> 0%
where the time goes in v1:
time: 93.1 us; the launch traced here: 92.9 us
  Pallas kernels  86.6 us (93%)
  local copies, waits for them, and re-layouts  5.03 us (5%)
  between operations  1.3 us (1%)
    pallas_call x1, Pallas kernels, per_device(): pl.pallas_call(functools.partial(fused_kernel, n, m, share, early), out_s...  86.6 us
    unnamed x8, local copies, waits for them, and re-layouts  3.76 us

profile of v1, /device:TPU:0, one launch (start us, length us, event | category | flops | bytes accessed | tf_op | source)
XLA Modules:
  0.0 92.9 jit_solution(11458975928068355349)
XLA Ops:
  1.3 86.6 %shard_map.93 = (bf16[256,1024]{1,0:T(8,128)(2,1)}, bf16[256,2048]{1,0:T(8,128)(2,1)}, f32[256,1024]{1,0:T(8,128)}) custom-call(s32[1]{0:T(128)S(6)} %copy.14.blk_ref, bf16[256,2048]{1,0:T(8,128)(2,1)} %bitcast.9, bf16[256,1024]{1,0:T(8,128)(2,1)} %bitcast.12, bf16[256,1024]{1,0:T(8,128)(2,1)} %bitcast.13, bf16[1024,128]{1,0:T(8,128)(2,1)} %wk_ref.1, ...), custom_call_target="tpu_custom_call" | custom-call | tf_op jit(solution)/shard_map/pallas_call | solution.py:293
  87.8 1.3 %slice_bitcast_fusion = (f32[1024,128]{0,1:T(8,128)S(1)}, f32[1024,128]{0,1:T(8,128)S(1)}) fusion(f32[256,1024]{1,0:T(8,128)} %get-tuple-element.9), kind=kLoop, calls=%fused_computation | loop fusion | bytes 2097152 | tf_op jit(solution)/shard_map/transpose | solution.py:342
  89.1 0.0 copy-start.1
  89.1 1.0 %copy.11 = f32[1024,128]{1,0:T(8,128)} copy(f32[1024,128]{0,1:T(8,128)S(1)} %get-tuple-element.14) | data formatting | bytes 1048576
  90.1 0.0 copy-start
  90.1 1.0 %copy.10 = f32[1024,128]{1,0:T(8,128)} copy(f32[1024,128]{0,1:T(8,128)S(1)} %get-tuple-element.15) | data formatting | bytes 1048576
  91.1 0.0 copy-done.1
  91.1 0.8 copy.15
  91.9 0.0 copy-done
  91.9 1.0 %copy.16 = bf16[1,2,128,2048]{3,2,1,0:T(8,128)(2,1)} copy(bf16[1,2,128,2048]{3,2,1,0:T(8,128)(2,1)S(1)} %bitcast.10) | data formatting | bytes 2097152
Async XLA Ops:
  89.1 2.0 %copy-start.1 = (bf16[256,1024]{1,0:T(8,128)(2,1)S(1)}, bf16[256,1024]{1,0:T(8,128)(2,1)}, u32[]{:S(2)}) copy-start(bf16[256,1024]{1,0:T(8,128)(2,1)} %get-tuple-element.7) | copy-start | bytes 1572868
  90.1 1.8 %copy-start = (bf16[256,2048]{1,0:T(8,128)(2,1)S(1)}, bf16[256,2048]{1,0:T(8,128)(2,1)}, u32[]{:S(2)}) copy-start(bf16[256,2048]{1,0:T(8,128)(2,1)} %get-tuple-element.8) | copy-start | bytes 3145732

commit v2 on v1

--- a/solution.py
+++ b/solution.py
@@ -34,7 +34,7 @@
 def fused_kernel(
     n, m, share, early,
     blk_ref, tok_ref, q_ref, g_ref, wk_ref, wv_ref,
-    dq_ref, gx_ref, gw_ref,
+    dq_ref, gx_ref, gwk_ref, gwv_ref,
     tokf, wf, wo, kv, kvn, kt, knt, dkv, dn, pgp, pin, pga, pgo, tokd, gsum, rp, rin, rall,
     loc_sem, tok_sem, wz_s, wz_r, wd_s, wd_r, wx_s, wx_r, wo_sem, kv_s, kv_r,
     td_s, td_r, tf_s, tf_r, pp_s, pp_r, pn_s, pn_r, pc_s, pc_r, po_sem, rs_s, rs_r, ra_s, ra_r,
@@ -59,13 +59,25 @@
     def put(src, dst, send_sem, recv_sem, **device):
         copy = copy_of(src, dst, send_sem, recv_sem, **device)
         copy.start()
-        sends.append(copy)
+        sends.append((None, copy))
+
+    def put_if(condition, src, dst, send_sem, recv_sem, **device):
+        copy = copy_of(src, dst, send_sem, recv_sem, **device)
+        pl.when(condition)(copy.start)
+        sends.append((condition, copy))
 
     def arrived(dst, send_sem, recv_sem):
         copy_of(dst, dst, send_sem, recv_sem, head=other).wait_recv()
 
     ctx_peers = [(off, lax.rem(me + off, n)) for off in near_first(n)]
     dp_peers = [(off, lax.rem(me_dp + off, m)) for off in near_first(m)]
+
+    two_step = m == 4 and share % 32 == 0
+    if two_step:
+        low = lax.rem(me_dp, 2)
+        w_peers = [(0, me_dp + 1 - 2 * low), (1, lax.rem(me_dp + 2, 4))]
+    else:
+        w_peers = [(at, peer) for at, (_, peer) in enumerate(dp_peers)]
 
     own_copies = [
         pltpu.make_async_copy(wk_ref, wf.at[me, :, pl.ds(0, HEAD_DIM)], loc_sem.at[0]),
@@ -108,14 +120,13 @@
         count = early if part == 0 else rows - early
         return pl.ds(pl.multiple_of(core * rows + start, 16), count)
 
-    def send_tokens(part):
+    def token_copy(part, off, peer):
         span = token_rows(head, part)
-        for off, peer in ctx_peers:
-            side, columns = token_block(peer)
-            put(
-                tokf.at[side, span, columns], tokd.at[me, span],
-                td_s.at[part, off], td_r.at[part, me], context=peer,
-            )
+        side, columns = token_block(peer)
+        return copy_of(
+            tokf.at[side, span, columns], tokd.at[me, span],
+            td_s.at[part, off], td_r.at[part, me], context=peer,
+        )
 
     my_side, my_columns = token_block(me)
     own_tokens = pltpu.make_async_copy(tokf.at[my_side, :, my_columns], tokd.at[me], loc_sem.at[3])
@@ -123,17 +134,42 @@
     for off, src in ctx_peers:
         part = wf.at[src, shared]
         arrived(part, wz_s.at[off], wz_r.at[src])
-        for dp_off, peer in dp_peers:
-            put(part, part, wx_s.at[src, dp_off], wx_r.at[src, me_dp], dp=peer)
-    send_tokens(0)
+        for dp_at, peer in w_peers:
+            put(part, part, wx_s.at[src, dp_at], wx_r.at[src, dp_at], dp=peer)
+    if two_step:
+        for off, src in ctx_peers:
+            for dp_at, peer in w_peers:
+                base = pl.multiple_of(peer * share, 16)
+                whole = wf.at[src, pl.ds(base, share)]
+                arrived(whole, wx_s.at[src, dp_at], wx_r.at[src, dp_at])
+                to = w_peers[1 - dp_at][1]
+                start = 0 if dp_at == 0 else share // 2
+                piece = wf.at[src, pl.ds(pl.multiple_of(base + start, 16), share // 2)]
+                put(piece, piece, wx_s.at[src, 2 + dp_at], wx_r.at[src, 2 + dp_at], dp=to)
+    for off, peer in ctx_peers:
+        copy = token_copy(0, off, peer)
+        copy.start()
+        sends.append((None, copy))
+    for off, peer in ctx_peers:
+        copy = token_copy(1, off, peer)
+        pl.when(peer < me)(copy.start)
+        sends.append((None, copy))
 
     projected = dot(tokf[my_side, :, my_columns], wf[me])
     for off, src in ctx_peers:
         if direct_rows:
             arrived(wf.at[src, direct], wd_s.at[off], wd_r.at[src])
-        for dp_off, peer in dp_peers:
-            theirs = pl.ds(pl.multiple_of(peer * share, 16), share)
-            arrived(wf.at[src, theirs], wx_s.at[src, dp_off], wx_r.at[src, peer])
+        if two_step:
+            base = (3 - me_dp) * share
+            for dp_at in range(2):
+                start = 0 if dp_at == 0 else share // 2
+                theirs = pl.ds(pl.multiple_of(base + start, 16), share // 2)
+                arrived(wf.at[src, theirs], wx_s.at[src, 2 + dp_at], wx_r.at[src, 2 + dp_at])
+        else:
+            for dp_at, peer in w_peers:
+                origin = lax.rem(me_dp + m - dp_peers[dp_at][0], m)
+                theirs = pl.ds(pl.multiple_of(origin * share, 16), share)
+                arrived(wf.at[src, theirs], wx_s.at[src, dp_at], wx_r.at[src, dp_at])
         side, columns = token_block(src)
         projected += dot(tokf[side, :, columns], wf[src])
     pairs = projected.astype(jnp.bfloat16)
@@ -141,9 +177,10 @@
     kv[my_rows, :] = pairs[:rows]
     kvn[...] = pairs[rows:]
     for off, peer in ctx_peers:
-        put(kv.at[my_rows], kv.at[my_rows], kv_s.at[off], kv_r.at[me], context=peer)
+        put_if(peer > me, kv.at[my_rows], kv.at[my_rows], kv_s.at[off], kv_r.at[me], context=peer)
     put(wf.at[pl.ds(other * half, half)], wo, wo_sem.at[0], wo_sem.at[1], head=other)
-    send_tokens(1)
+    for off, peer in ctx_peers:
+        pl.when(peer > me)(token_copy(1, off, peer).start)
 
     block = blk_ref[0]
     total_rows = n * rows
@@ -157,7 +194,14 @@
     knt[...] = kvn[:, :HEAD_DIM].T
     for off, src in ctx_peers:
         span = pl.ds(pl.multiple_of(src * rows, rows), rows)
-        arrived(kv.at[span], kv_s.at[off], kv_r.at[src])
+
+        @pl.when(src < me)
+        def _(span=span, off=off, src=src):
+            arrived(kv.at[span], kv_s.at[off], kv_r.at[src])
+
+        @pl.when(src > me)
+        def _(span=span):
+            kv[span, :] = jnp.zeros((rows, 2 * HEAD_DIM), jnp.bfloat16)
     kt[...] = kv[:, :HEAD_DIM].T
 
     def head_turn(turn, carry):
@@ -213,17 +257,21 @@
         pgp[block_at] = (dkv[block_at * rows : (block_at + 1) * rows] * pair_scale).astype(jnp.bfloat16)
     clean, noisy = pl.ds(0, rows), pl.ds(rows, rows)
     for off, peer in ctx_peers:
-        put(pgp.at[peer], pin.at[me], pp_s.at[off], pp_r.at[me], context=peer)
+        put_if(peer < me, pgp.at[peer], pin.at[me], pp_s.at[off], pp_r.at[me], context=peer)
     pga[me, noisy] = (dn[...] * pair_scale).astype(jnp.bfloat16)
     part = pga.at[me, noisy]
     put(part, pgo.at[noisy], po_sem.at[0], po_sem.at[1], head=other)
     for off, peer in ctx_peers:
         put(part, part, pn_s.at[off], pn_r.at[me], context=peer)
-    clean_sum = dkv[my_rows, :] * pair_scale
-    for off, src in ctx_peers:
-        arrived(pin.at[src], pp_s.at[off], pp_r.at[src])
-        clean_sum += pin[src].astype(jnp.float32)
-    pga[me, clean] = clean_sum.astype(jnp.bfloat16)
+    dkv[my_rows, :] *= pair_scale
+    for off, src in ctx_peers:
+
+        @pl.when(src > me)
+        def _(off=off, src=src):
+            arrived(pin.at[src], pp_s.at[off], pp_r.at[src])
+            dkv[my_rows, :] += pin[src].astype(jnp.float32)
+
+    pga[me, clean] = dkv[my_rows, :].astype(jnp.bfloat16)
     part = pga.at[me, clean]
     for off, peer in ctx_peers:
         put(part, part, pc_s.at[off], pc_r.at[me], context=peer)
@@ -270,9 +318,14 @@
     for off, src in dp_peers:
         arrived(rall.at[src], ra_s.at[off], ra_r.at[src])
     for at in range(m):
-        gw_ref[at * slab : (at + 1) * slab] = rall[at].astype(jnp.float32)
-    for copy in sends:
-        copy.wait_send()
+        gsum[at] = rall[at].astype(jnp.float32)
+    gwk_ref[...] = gsum[: m // 2].reshape(HEAD_DIM, wrows).T
+    gwv_ref[...] = gsum[m // 2 :].reshape(HEAD_DIM, wrows).T
+    for condition, copy in sends:
+        if condition is None:
+            copy.wait_send()
+        else:
+            pl.when(condition)(copy.wait_send)
 
 
 def per_device(tokens, queries, grad_out, w_key, w_value, block_len):
@@ -282,23 +335,24 @@
     features = tokens.shape[3]
     wrows, width = w_key.shape
     q_width = queries.shape[3]
-    share = wrows * 7 // 8 // m // 16 * 16
-    early = rows // 2
+    share = wrows // m // 16 * 16
+    early = min(16, rows // 2)
     half = n // 2
     pair = 2 * width
     bf16, f32 = jnp.bfloat16, jnp.float32
     vmem = pl.BlockSpec(memory_space=pltpu.VMEM)
     dma = pltpu.SemaphoreType.DMA
     slab = pair // m
-    dq, gx, gw = pl.pallas_call(
+    dq, gx, gwk, gwv = pl.pallas_call(
         functools.partial(fused_kernel, n, m, share, early),
         out_shape=(
             jax.ShapeDtypeStruct((2 * rows, q_width), bf16),
             jax.ShapeDtypeStruct((2 * rows, features), bf16),
-            jax.ShapeDtypeStruct((pair, wrows), f32),
+            jax.ShapeDtypeStruct((wrows, width), f32),
+            jax.ShapeDtypeStruct((wrows, width), f32),
         ),
         in_specs=[pl.BlockSpec(memory_space=pltpu.SMEM)] + [vmem] * 5,
-        out_specs=(vmem, vmem, vmem),
+        out_specs=(vmem, vmem, vmem, vmem),
         scratch_shapes=[
             pltpu.VMEM((2, 2 * rows, features), bf16),
             pltpu.VMEM((n, wrows, pair), bf16),
@@ -338,8 +392,8 @@
     return (
         dq.reshape(queries.shape),
         gx.reshape(tokens.shape),
-        gw[:width].T,
-        gw[width:].T,
+        gwk,
+        gwv,
     )
 
 

time: 93.1 us -> 88 us (0.945)
  the two profiles are of different devices: /device:TPU:0 before, /device:TPU:24 now
where the time goes in v2:
time: 88 us; the launch traced here: 87.7 us
  Pallas kernels  81 us (92%)
  local copies, waits for them, and re-layouts  5.38 us (6%)
  between operations  1.3 us (1%)
    pallas_call x1, Pallas kernels, per_device(): pl.pallas_call(functools.partial(fused_kernel, n, m, share, early), out_s...  81 us
    unnamed x10, local copies, waits for them, and re-layouts  5.38 us

profile of v2, /device:TPU:24, one launch (start us, length us, event | category | flops | bytes accessed | tf_op | source)
XLA Modules:
  0.0 87.7 jit_solution(13553537392901175989)
XLA Ops:
  1.3 81.0 %shard_map.93 = (bf16[256,1024]{1,0:T(8,128)(2,1)}, bf16[256,2048]{1,0:T(8,128)(2,1)}, f32[1024,128]{1,0:T(8,128)}, f32[1024,128]{1,0:T(8,128)}) custom-call(s32[1]{0:T(128)S(6)} %copy.14.blk_ref, bf16[256,2048]{1,0:T(8,128)(2,1)} %bitcast.5, bf16[256,1024]{1,0:T(8,128)(2,1)} %bitcast.8, bf16[256,1024]{1,0:T(8,128)(2,1)} %bitcast.9, ...), custom_call_target="tpu_custom_call" | custom-call | tf_op jit(solution)/shard_map/pallas_call | solution.py:346
  82.3 0.0 copy-start
  82.3 2.0 %copy.15 = bf16[1,2,128,1024]{3,2,1,0:T(8,128)(2,1)} copy(bf16[1,2,128,1024]{3,2,1,0:T(8,128)(2,1)} %bitcast.7) | data formatting | bytes 1048576
  84.2 0.0 copy-done
  84.2 0.0 copy-start.2
  84.2 1.0 %copy.16 = bf16[1,2,128,2048]{3,2,1,0:T(8,128)(2,1)} copy(bf16[1,2,128,2048]{3,2,1,0:T(8,128)(2,1)S(1)} %bitcast.6) | data formatting | bytes 2097152
  85.2 0.4 copy-done.2
  85.6 0.0 copy-start.1
  85.6 0.8 copy.17
  86.4 0.4 copy-done.1
  86.9 0.8 copy.18
Async XLA Ops:
  82.3 2.0 %copy-start = (bf16[256,2048]{1,0:T(8,128)(2,1)S(1)}, bf16[256,2048]{1,0:T(8,128)(2,1)}, u32[]{:S(2)}) copy-start(bf16[256,2048]{1,0:T(8,128)(2,1)} %get-tuple-element.9) | copy-start | bytes 3145732
  84.2 1.4 %copy-start.2 = (f32[1024,128]{1,0:T(8,128)S(1)}, f32[1024,128]{1,0:T(8,128)}, u32[]{:S(2)}) copy-start(f32[1024,128]{1,0:T(8,128)} %get-tuple-element.18) | copy-start | bytes 1572868
  85.6 1.2 %copy-start.1 = (f32[1024,128]{1,0:T(8,128)S(1)}, f32[1024,128]{1,0:T(8,128)}, u32[]{:S(2)}) copy-start(f32[1024,128]{1,0:T(8,128)} %get-tuple-element.19) | copy-start | bytes 1572868

commit v3 on v2

--- a/solution.py
+++ b/solution.py
@@ -336,7 +336,7 @@
     wrows, width = w_key.shape
     q_width = queries.shape[3]
     share = wrows // m // 16 * 16
-    early = min(16, rows // 2)
+    early = max(16, rows // 64 * 16)
     half = n // 2
     pair = 2 * width
     bf16, f32 = jnp.bfloat16, jnp.float32

time: 88 us -> 86.5 us (0.983)
  the two profiles are of different devices: /device:TPU:24 before, /device:TPU:0 now
where the time goes in v3:
time: 86.5 us; the launch traced here: 85.7 us
  Pallas kernels  79 us (91%)
  local copies, waits for them, and re-layouts  5.38 us (6%)
  between operations  1.3 us (2%)
    pallas_call x1, Pallas kernels, per_device(): pl.pallas_call(functools.partial(fused_kernel, n, m, share, early), out_s...  79 us
    unnamed x10, local copies, waits for them, and re-layouts  5.38 us

profile of v3, /device:TPU:0, one launch (start us, length us, event | category | flops | bytes accessed | tf_op | source)
XLA Modules:
  0.0 85.7 jit_solution(9605043799375072434)
XLA Ops:
  1.3 79.0 %shard_map.93 = (bf16[256,1024]{1,0:T(8,128)(2,1)}, bf16[256,2048]{1,0:T(8,128)(2,1)}, f32[1024,128]{1,0:T(8,128)}, f32[1024,128]{1,0:T(8,128)}) custom-call(s32[1]{0:T(128)S(6)} %copy.14.blk_ref, bf16[256,2048]{1,0:T(8,128)(2,1)} %bitcast.5, bf16[256,1024]{1,0:T(8,128)(2,1)} %bitcast.8, bf16[256,1024]{1,0:T(8,128)(2,1)} %bitcast.9, ...), custom_call_target="tpu_custom_call" | custom-call | tf_op jit(solution)/shard_map/pallas_call | solution.py:346
  80.3 0.0 copy-start
  80.3 2.0 %copy.15 = bf16[1,2,128,1024]{3,2,1,0:T(8,128)(2,1)} copy(bf16[1,2,128,1024]{3,2,1,0:T(8,128)(2,1)} %bitcast.7) | data formatting | bytes 1048576
  82.3 0.0 copy-done
  82.3 0.0 copy-start.2
  82.3 1.0 %copy.16 = bf16[1,2,128,2048]{3,2,1,0:T(8,128)(2,1)} copy(bf16[1,2,128,2048]{3,2,1,0:T(8,128)(2,1)S(1)} %bitcast.6) | data formatting | bytes 2097152
  83.3 0.4 copy-done.2
  83.7 0.0 copy-start.1
  83.7 0.8 copy.17
  84.5 0.4 copy-done.1
  84.9 0.8 copy.18
Async XLA Ops:
  80.3 2.0 %copy-start = (bf16[256,2048]{1,0:T(8,128)(2,1)S(1)}, bf16[256,2048]{1,0:T(8,128)(2,1)}, u32[]{:S(2)}) copy-start(bf16[256,2048]{1,0:T(8,128)(2,1)} %get-tuple-element.9) | copy-start | bytes 3145732
  82.3 1.4 %copy-start.2 = (f32[1024,128]{1,0:T(8,128)S(1)}, f32[1024,128]{1,0:T(8,128)}, u32[]{:S(2)}) copy-start(f32[1024,128]{1,0:T(8,128)} %get-tuple-element.18) | copy-start | bytes 1572868
  83.7 1.2 %copy-start.1 = (f32[1024,128]{1,0:T(8,128)S(1)}, f32[1024,128]{1,0:T(8,128)}, u32[]{:S(2)}) copy-start(f32[1024,128]{1,0:T(8,128)} %get-tuple-element.19) | copy-start | bytes 1572868
